TPU v7x, 32 devices: a whole 2x2x4 slice. The times are simulated.
32 devices in a mesh: layer: 4 (over y, x), row: 2 (over core), col: 4 (over z).
Axes of the slice: x: 2, y: 2, z: 4, core: 2. Of those that a mesh axis runs over, the one named last changes fastest.
Arguments:
- block_values: bfloat16 [4, 2, 4, 32, 256, 256], P('layer', 'row', 'col'), may hold values from 0 to 3
- block_rows: int32 [4, 2, 4, 32], P('layer', 'row', 'col'), may hold values from 0 to 255
- block_cols: int32 [4, 2, 4, 32], P('layer', 'row', 'col'), may hold values from 0 to 127
- block_count: int32 [4, 2, 4], P('layer', 'row', 'col'), may hold values from 1 to 32, as said below
- dangling: int32 [4, 2, 4, 16384], P('layer', 'row', 'col'), may hold values 0 or 1
- start_ranks: float32 [4, 2, 4, 16384], P('layer', 'row', 'col'), may hold values from 0.2 to 5
Outputs:
- ranks: float32 [4, 2, 4, 16384], P('layer', 'row', 'col')
- residuals: float32 [3, 4], P(None, 'layer')
Inputs may be any that keep to these rules, and one draw needn't show every extreme that they name: `block_count`: live slots of a tile; in every layer some tile has all 32 slots live. `block_rows`: slots at or past a tile's count carry no edges; coordinates may repeat within a tile, and repeated blocks add.
All inputs are finite; a program needn't handle non-finite values. No bound on the sum of `dangling` on one device may be relied on, other than what follows from the above.
Results may differ from a plain program's by a relative error of at most 0.0012.
Values may be sent and summed in bfloat16 or wider, within the bound.
A program may use at most 64 MiB of HBM per device.

v0:
```python
import jax
import jax.numpy as jnp
from jax import lax
from jax.sharding import PartitionSpec as P

ITERS = 3
damping = 0.85
coupling = 0.3


def with_halo(x, sides, width):
    for axis, dim in sides:
        count, length = (lax.axis_size(axis), x.shape[dim])
        up = [(i, (i + 1) % count) for i in range(count - 1)]
        down = [(j, i) for i, j in up]
        last = lax.slice_in_dim(x, length - width, length, axis=dim)
        first = lax.slice_in_dim(x, 0, width, axis=dim)
        before = lax.ppermute(last, axis, up)
        after = lax.ppermute(first, axis, down)
        x = jnp.concatenate([before, x, after], axis=dim)
    return x


def block_terms(values, rows_here, cols_here, live_here, column_bf, row_blk):
    picked = jnp.take(column_bf, cols_here, axis=0)
    products = jnp.einsum("sij,sj->si", values, picked, preferred_element_type=jnp.float32)
    onehot = (rows_here[:, None] == jnp.arange(row_blk)[None, :]).astype(jnp.float32) * live_here[
        :, None
    ]
    return jnp.einsum("sb,si->bi", onehot, products, precision=lax.Precision.HIGHEST)


def layer_walk(values, rows_here, cols_here, live_here, column_bf, row_blk):
    return block_terms(values, rows_here, cols_here, live_here, column_bf, row_blk)


def local(block_values, block_rows, block_cols, block_count, dangling, start_ranks):
    layer_dev = start_ranks.shape[0]
    span_len = start_ranks.shape[-1]
    row_devices = lax.axis_size("row")
    col_devices = lax.axis_size("col")
    block_edge = block_values.shape[-1]
    slots = block_values.shape[3]
    col_blk = row_devices * span_len // block_edge
    row_blk = col_devices * span_len // block_edge
    node_total = row_devices * col_devices * span_len
    layers = layer_dev * lax.axis_size("layer")
    values = block_values[:, 0, 0]
    block_row = block_rows[:, 0, 0]
    block_col = block_cols[:, 0, 0]
    counts = block_count[:, 0, 0]
    live_slot = (jnp.arange(slots)[None, :] < counts[:, None]).astype(jnp.float32)
    colsum = jnp.einsum(
        "lsij,i->lsj",
        values,
        jnp.ones((block_edge,), jnp.bfloat16),
        preferred_element_type=jnp.float32,
    )
    onehot = (block_col[..., None] == jnp.arange(col_blk)[None, None, :]).astype(
        jnp.float32
    ) * live_slot[..., None]
    deg_part = jnp.einsum("lsb,lsj->lbj", onehot, colsum, precision=lax.Precision.HIGHEST)
    deg_part = deg_part.reshape(layer_dev, row_devices, 1, span_len)
    degree = lax.psum(deg_part, "row")
    own_degree = lax.dynamic_slice_in_dim(degree, lax.axis_index("row"), 1, 1)
    keep_mask = 1.0 - dangling.astype(jnp.float32)
    own_denominator = keep_mask * own_degree + 1.0
    layer_ids = lax.axis_index("layer") * layer_dev + jnp.arange(layer_dev)
    spread = (
        jnp.where((layer_ids == 0) | (layer_ids == layers - 1), 1.0, 0.5).astype(jnp.float32)
        * coupling
    )
    spread = spread.reshape(layer_dev, 1, 1, 1)
    ranks_now = start_ranks
    residual_list = []
    for iteration in range(ITERS):
        spill = ranks_now * spread
        padded = with_halo(spill.astype(jnp.bfloat16), (("layer", 0),), 1).astype(spill.dtype)
        arrive = padded[:-2] + padded[2:]
        scaled_own = (ranks_now * keep_mask / own_denominator).astype(jnp.bfloat16)
        column_vec = lax.all_gather(scaled_own, "row", axis=1, tiled=True)
        dangle_mass = lax.psum(jnp.sum(ranks_now / own_denominator, axis=(1, 2, 3)), ("row", "col"))
        scaled = column_vec.reshape(layer_dev, col_blk, block_edge)
        layer_terms = [
            layer_walk(values[0], block_row[0], block_col[0], live_slot[0], scaled[0], row_blk)
        ]
        partial_value = jnp.stack(layer_terms).reshape(layer_dev, 1, col_devices, span_len)
        whole = lax.psum(partial_value, "col")
        walk_sum = lax.dynamic_slice_in_dim(whole, lax.axis_index("col"), 1, 2)
        updated = damping * (
            (1.0 - coupling) * (walk_sum + dangle_mass.reshape(layer_dev, 1, 1, 1) / node_total)
            + arrive
        ) + (1.0 - damping)
        change = jnp.sum(jnp.abs(updated - ranks_now), axis=(1, 2, 3))
        change_total = lax.psum(change, ("row", "col"))
        residual_list.append(change_total)
        ranks_now = updated
    return (ranks_now, jnp.stack(residual_list))


def solution(mesh):
    placed = (
        P("layer", "row", "col", None, None, None),
        P("layer", "row", "col", None),
        P("layer", "row", "col", None),
        P("layer", "row", "col"),
        P("layer", "row", "col", None),
        P("layer", "row", "col", None),
    )
    return jax.shard_map(
        local,
        mesh=mesh,
        in_specs=placed,
        out_specs=(P("layer", "row", "col", None), P(None, "layer")),
        check_vma=False,
    )
```

profile of v0, /device:TPU:1, one launch (start us, length us, event | category | flops | bytes accessed | tf_op | source)
XLA Modules:
  0.0 197.9 jit_solution(1086443442296965706)
XLA Ops:
  7.9 2.8 %fusion.6 = f32[1,32,256]{2,0,1:T(1,128)S(1)} fusion(bf16[1,1,1,32,256,256]{5,4,3,2,1,0:T(8,128)(2,1)} %param.8), kind=kOutput, calls=%fused_computation.9 | convolution fusion | flops 4194304 | bytes 4227072 | tf_op jit(solution)/shard_map/lsij,i->lsj/dot_general | solution.py:53
  12.1 20.4 %all-reduce.6.cloned.1.call-done = f32[1,2,1,16384]{3,2,0,1:T(1,128)} async-done(((f32[1,2,1,16384]{3,2,0,1:T(1,128)}), f32[1,2,1,16384]{3,2,0,1:T(1,128)}) %all-reduce.6.cloned.1.call-update) | async-done | bytes 131088 | tf_op jit(solution)/shard_map/psum | solution.py:64
  32.6 1.6 fusion.20
  34.3 1.9 all_gather.9
  37.3 3.4 %fusion.4 = f32[32,1,256]{2,1,0:T(1,128)S(1)} fusion(bf16[1,1,1,32,256,256]{5,4,3,2,1,0:T(8,128)(2,1)} %param.8, bf16[32,256,1]{1,0,2:T(8,128)(2,1)S(1)} %select_bitcast_fusion.2), kind=kOutput, calls=%fused_computation.7 | convolution fusion | flops 4194304 | bytes 4243456 | tf_op jit(solution)/shard_map/sij,sj->si/dot_general | solution.py:26
  42.2 3.4 %collective-permute-start = (bf16[1,1,1,16384]{3,2,0,1:T(2,128)(2,1)S(1)}, bf16[1,1,1,16384]{3,2,0,1:T(2,128)(2,1)S(1)}, u32[]{:S(2)}, u32[]{:S(2)}) collective-permute-start(bf16[1,1,1,16384]{3,2,0,1:T(2,128)(2,1)S(1)} %bitcast_convert_fusion), channel_id=1, source_target_pairs={{0,8},{8,16},{16,24},{1,9},{9,17},{17,25},{2,10},{10,18},{18,26},{... | collective-permute-start | bytes 98312 | tf_op jit(solution)/shard_map/ppermute | solution.py:18
  45.6 1.3 collective-permute-start.1
  46.9 17.9 %psum.72 = f32[1]{0:T(128)} all-reduce(f32[1]{0:T(128)} %bitcast.11), channel_id=1, replica_groups=mesh['layer'=4,'row'=2,'col'=4] {'row','col'}, use_global_device_ids=true, to_apply=%region_3.5 | all-reduce | flops 1 | bytes 8 | tf_op jit(solution)/shard_map/psum | solution.py:82
  65.4 11.0 %all-reduce.8.cloned.1.call-done = f32[1,1,4,16384]{3,2,0,1:T(4,128)} async-done(((f32[1,1,4,16384]{3,2,0,1:T(4,128)}), f32[1,1,4,16384]{3,2,0,1:T(4,128)}) %all-reduce.8.cloned.1.call-update) | async-done | bytes 262160 | tf_op jit(solution)/shard_map/psum | solution.py:88
  76.4 1.8 divide_reduce_fusion.1
  78.4 4.3 %all_gather.10 = bf16[1,2,1,16384]{3,2,0,1:T(2,128)(2,1)S(1)} all-gather(bf16[1,1,1,16384]{3,2,0,1:T(2,128)(2,1)S(1)} %get-tuple-element.22), channel_id=1, replica_groups=mesh['layer'=4,'row'=2,'col'=4] {'row'}, dimensions={1}, use_global_device_ids=true | all-gather | bytes 98304 | tf_op jit(solution)/shard_map/all_gather | solution.py:81
  83.9 3.4 %fusion.2 = f32[32,1,256]{2,1,0:T(1,128)S(1)} fusion(bf16[1,1,1,32,256,256]{5,4,3,2,1,0:T(8,128)(2,1)} %param.8, bf16[32,256,1]{1,0,2:T(8,128)(2,1)S(1)} %select_bitcast_fusion.1), kind=kOutput, calls=%fused_computation.5 | convolution fusion | flops 4194304 | bytes 4243456 | tf_op jit(solution)/shard_map/sij,sj->si/dot_general | solution.py:26
  88.6 3.1 %collective-permute-start.2 = (bf16[1,1,1,16384]{3,2,0,1:T(2,128)(2,1)S(1)}, bf16[1,1,1,16384]{3,2,0,1:T(2,128)(2,1)S(1)}, u32[]{:S(2)}, u32[]{:S(2)}) collective-permute-start(bf16[1,1,1,16384]{3,2,0,1:T(2,128)(2,1)S(1)} %get-tuple-element.23), channel_id=1, source_target_pairs={{0,8},{8,16},{16,24},{1,9},{9,17},{17,25},{2,10},{10,18},{18,26},{... | collective-permute-start | bytes 98312 | tf_op jit(solution)/shard_map/ppermute | solution.py:18
  93.0 17.0 %psum.74 = f32[1]{0:T(128)} all-reduce(f32[1]{0:T(128)} %bitcast.18), channel_id=1, replica_groups=mesh['layer'=4,'row'=2,'col'=4] {'row','col'}, use_global_device_ids=true, to_apply=%region_6.8 | all-reduce | flops 1 | bytes 8 | tf_op jit(solution)/shard_map/psum | solution.py:82
  110.7 11.1 %all-reduce.10.cloned.1.call-done = f32[1,1,4,16384]{3,2,0,1:T(4,128)} async-done(((f32[1,1,4,16384]{3,2,0,1:T(4,128)}), f32[1,1,4,16384]{3,2,0,1:T(4,128)}) %all-reduce.10.cloned.1.call-update) | async-done | bytes 262160 | tf_op jit(solution)/shard_map/psum | solution.py:88
  121.8 1.8 divide_reduce_fusion
  123.8 4.3 %all_gather.11 = bf16[1,2,1,16384]{3,2,0,1:T(2,128)(2,1)S(1)} all-gather(bf16[1,1,1,16384]{3,2,0,1:T(2,128)(2,1)S(1)} %get-tuple-element.20), channel_id=1, replica_groups=mesh['layer'=4,'row'=2,'col'=4] {'row'}, dimensions={1}, use_global_device_ids=true | all-gather | bytes 98304 | tf_op jit(solution)/shard_map/all_gather | solution.py:81
  129.3 3.4 %fusion = f32[32,1,256]{2,1,0:T(1,128)S(1)} fusion(bf16[1,1,1,32,256,256]{5,4,3,2,1,0:T(8,128)(2,1)} %param.8, bf16[32,256,1]{1,0,2:T(8,128)(2,1)S(1)} %select_bitcast_fusion), kind=kOutput, calls=%fused_computation.3 | convolution fusion | flops 4194304 | bytes 4243456 | tf_op jit(solution)/shard_map/sij,sj->si/dot_general | solution.py:26
  134.0 3.1 %collective-permute-start.4 = (bf16[1,1,1,16384]{3,2,0,1:T(2,128)(2,1)S(1)}, bf16[1,1,1,16384]{3,2,0,1:T(2,128)(2,1)S(1)}, u32[]{:S(2)}, u32[]{:S(2)}) collective-permute-start(bf16[1,1,1,16384]{3,2,0,1:T(2,128)(2,1)S(1)} %get-tuple-element.21), channel_id=1, source_target_pairs={{0,8},{8,16},{16,24},{1,9},{9,17},{17,25},{2,10},{10,18},{18,26},{... | collective-permute-start | bytes 98312 | tf_op jit(solution)/shard_map/ppermute | solution.py:18
  138.4 16.9 %psum.76 = f32[1]{0:T(128)} all-reduce(f32[1]{0:T(128)} %bitcast.23), channel_id=1, replica_groups=mesh['layer'=4,'row'=2,'col'=4] {'row','col'}, use_global_device_ids=true, to_apply=%region_9.11 | all-reduce | flops 1 | bytes 8 | tf_op jit(solution)/shard_map/psum | solution.py:82
  156.0 11.2 %all-reduce.12.cloned.1.call-done = f32[1,1,4,16384]{3,2,0,1:T(4,128)} async-done(((f32[1,1,4,16384]{3,2,0,1:T(4,128)}), f32[1,1,4,16384]{3,2,0,1:T(4,128)}) %all-reduce.12.cloned.1.call-update) | async-done | bytes 262160 | tf_op jit(solution)/shard_map/psum | solution.py:88
  167.2 2.6 %fusion.19 = (f32[]{:T(128)}, f32[]{:T(128)}, f32[]{:T(128)}, f32[1,1,1,16384]{3,2,0,1:T(1,128)}) fusion(f32[1,1,1,16384]{3,2,0,1:T(1,128)S(1)} %get-tuple-element.17, f32[1,1,1,16384]{3,2,1,0:T(1,128)S(1)} %copy-done.1, f32[1,1,1,16384]{3,2,0,1:T(1,128)S(1)} %get-tuple-element.15, bf16[1,1,1,16384]{3,2,0,1:T(2,128)(2,1)S(1)} %collective-permute-done.5, ...), kind=kLoop, calls=%fused_computation.43 | loop fusion | flops 344061 | bytes 426004 | tf_op jit(solution)/shard_map/reduce_sum | solution.py:94
  169.9 19.0 %all-reduce = (f32[1,1]{0,1:T(1,128)}, f32[1,1]{0,1:T(1,128)}, f32[1,1]{0,1:T(1,128)}) all-reduce(f32[1,1]{0,1:T(1,128)} %bitcast.29, f32[1,1]{0,1:T(1,128)} %bitcast.28, f32[1,1]{0,1:T(1,128)} %bitcast.27), channel_id=1, replica_groups=mesh['layer'=4,'row'=2,'col'=4] {'row','col'}, use_global_device_ids=true, to_apply=%region_15.17 | all-reduce | flops 3 | bytes 24 | tf_op jit(solution)/shard_map/psum | solution.py:95
  188.9 2.5 %pad_maximum_fusion.6 = f32[3,1]{0,1:T(1,128)} fusion(f32[1,1]{0,1:T(1,128)} %get-tuple-element.10, f32[1,1]{0,1:T(1,128)} %get-tuple-element.11, f32[1,1]{0,1:T(1,128)} %get-tuple-element.12), kind=kLoop, calls=%fused_computation.90 | loop fusion | flops 6 | bytes 24 | tf_op jit(solution)/shard_map/stack | solution.py:98
  (52 shorter events, 12.0 us)
Async XLA Ops:
  7.2 3.6 %copy-start.3 = (s32[1,1,1,32]{3,2,1,0:T(1,128)S(1)}, s32[1,1,1,32]{3,2,1,0:T(1,128)}, u32[]{:S(2)}) copy-start(s32[1,1,1,32]{3,2,1,0:T(1,128)} %param.10) | copy-start | bytes 388
  7.2 25.4 %copy-start = (s32[1,1,1,16384]{3,2,1,0:T(1,128)S(1)}, s32[1,1,1,16384]{3,2,1,0:T(1,128)}, u32[]{:S(2)}) copy-start(s32[1,1,1,16384]{3,2,1,0:T(1,128)} %param.12) | copy-start | bytes 196612
  7.2 25.4 %copy-start.1 = (f32[1,1,1,16384]{3,2,1,0:T(1,128)S(1)}, f32[1,1,1,16384]{3,2,1,0:T(1,128)}, u32[]{:S(2)}) copy-start(f32[1,1,1,16384]{3,2,1,0:T(1,128)} %param.13) | copy-start | bytes 196612
  7.2 25.4 %all-reduce.6.cloned.1.call-start = ((), (), s32[]{:S(2)}) async-start(), calls=%async_computation | async-start | bytes 262144 | tf_op jit(solution)/shard_map/psum | solution.py:64
  7.9 32.8 %copy-start.2 = (s32[1,1,1,32]{3,2,1,0:T(1,128)S(1)}, s32[1,1,1,32]{3,2,1,0:T(1,128)}, u32[]{:S(2)}) copy-start(s32[1,1,1,32]{3,2,1,0:T(1,128)} %param.9) | copy-start | bytes 388
  12.0 64.4 %all-reduce.8.cloned.1.call-start = ((), (), s32[]{:S(2)}) async-start(), calls=%async_computation.1 | async-start | bytes 524288 | tf_op jit(solution)/shard_map/psum | solution.py:88
  42.1 79.7 %all-reduce.10.cloned.1.call-start = ((), (), s32[]{:S(2)}) async-start(), calls=%async_computation.2 | async-start | bytes 524288 | tf_op jit(solution)/shard_map/psum | solution.py:88
  42.2 23.2 %collective-permute-start = (bf16[1,1,1,16384]{3,2,0,1:T(2,128)(2,1)S(1)}, bf16[1,1,1,16384]{3,2,0,1:T(2,128)(2,1)S(1)}, u32[]{:S(2)}, u32[]{:S(2)}) collective-permute-start(bf16[1,1,1,16384]{3,2,0,1:T(2,128)(2,1)S(1)} %bitcast_convert_fusion), channel_id=1, source_target_pairs={{0,8},{8,16},{16,24},{1,9},{9,17},{17,25},{2,10},{10,18},{18,26},{... | collective-permute-start | bytes 98312 | tf_op jit(solution)/shard_map/ppermute | solution.py:18
  45.6 19.8 %collective-permute-start.1 = (bf16[1,1,1,16384]{3,2,0,1:T(2,128)(2,1)S(1)}, bf16[1,1,1,16384]{3,2,0,1:T(2,128)(2,1)S(1)}, u32[]{:S(2)}, u32[]{:S(2)}) collective-permute-start(bf16[1,1,1,16384]{3,2,0,1:T(2,128)(2,1)S(1)} %bitcast_convert_fusion), channel_id=1, source_target_pairs={{8,0},{16,8},{24,16},{9,1},{17,9},{25,17},{10,2},{18,10},{26,18},{... | collective-permute-start | bytes 98312 | tf_op jit(solution)/shard_map/ppermute | solution.py:19
  88.6 78.6 %all-reduce.12.cloned.1.call-start = ((), (), s32[]{:S(2)}) async-start(), calls=%async_computation.3 | async-start | bytes 524288 | tf_op jit(solution)/shard_map/psum | solution.py:88
  88.6 22.1 %collective-permute-start.2 = (bf16[1,1,1,16384]{3,2,0,1:T(2,128)(2,1)S(1)}, bf16[1,1,1,16384]{3,2,0,1:T(2,128)(2,1)S(1)}, u32[]{:S(2)}, u32[]{:S(2)}) collective-permute-start(bf16[1,1,1,16384]{3,2,0,1:T(2,128)(2,1)S(1)} %get-tuple-element.23), channel_id=1, source_target_pairs={{0,8},{8,16},{16,24},{1,9},{9,17},{17,25},{2,10},{10,18},{18,26},{... | collective-permute-start | bytes 98312 | tf_op jit(solution)/shard_map/ppermute | solution.py:18
  91.7 19.0 %collective-permute-start.3 = (bf16[1,1,1,16384]{3,2,0,1:T(2,128)(2,1)S(1)}, bf16[1,1,1,16384]{3,2,0,1:T(2,128)(2,1)S(1)}, u32[]{:S(2)}, u32[]{:S(2)}) collective-permute-start(bf16[1,1,1,16384]{3,2,0,1:T(2,128)(2,1)S(1)} %get-tuple-element.23), channel_id=1, source_target_pairs={{8,0},{16,8},{24,16},{9,1},{17,9},{25,17},{10,2},{18,10},{26,18},{... | collective-permute-start | bytes 98312 | tf_op jit(solution)/shard_map/ppermute | solution.py:19
  134.0 22.0 %collective-permute-start.4 = (bf16[1,1,1,16384]{3,2,0,1:T(2,128)(2,1)S(1)}, bf16[1,1,1,16384]{3,2,0,1:T(2,128)(2,1)S(1)}, u32[]{:S(2)}, u32[]{:S(2)}) collective-permute-start(bf16[1,1,1,16384]{3,2,0,1:T(2,128)(2,1)S(1)} %get-tuple-element.21), channel_id=1, source_target_pairs={{0,8},{8,16},{16,24},{1,9},{9,17},{17,25},{2,10},{10,18},{18,26},{... | collective-permute-start | bytes 98312 | tf_op jit(solution)/shard_map/ppermute | solution.py:18
  137.1 18.9 %collective-permute-start.5 = (bf16[1,1,1,16384]{3,2,0,1:T(2,128)(2,1)S(1)}, bf16[1,1,1,16384]{3,2,0,1:T(2,128)(2,1)S(1)}, u32[]{:S(2)}, u32[]{:S(2)}) collective-permute-start(bf16[1,1,1,16384]{3,2,0,1:T(2,128)(2,1)S(1)} %get-tuple-element.21), channel_id=1, source_target_pairs={{8,0},{16,8},{24,16},{9,1},{17,9},{25,17},{10,2},{18,10},{26,18},{... | collective-permute-start | bytes 98312 | tf_op jit(solution)/shard_map/ppermute | solution.py:19
Sparse Core Ops, SparseCore 0:
  12.1 20.3 all-reduce.5
  42.2 34.1 all-reduce.7
  88.7 33.0 all-reduce.9
  134.1 33.0 all-reduce.11
where the time goes:
time: 199 us; the launch traced here: 198 us
  blocking collectives  81.3 us (41%)
  waiting for transfers between devices  53.8 us (27%)
  between operations  16.7 us (8%)
  matrix products  14.8 us (7%)
  starting transfers between devices  13.6 us (7%)
  other arithmetic  12.3 us (6%)
  local copies, waits for them, and re-layouts  5.32 us (3%)
    psum x3, blocking collectives, local(): lax.psum(jnp.sum(ranks_now / own_denominator, axis=(1, 2, 3)), ('row', 'c...  51.8 us
    psum x3, waiting for transfers between devices, local(): whole = lax.psum(partial_value, 'col')  33.3 us
    psum x1, waiting for transfers between devices, local(): degree = lax.psum(deg_part, 'row')  20.4 us
    psum x1, blocking collectives, local(): change_total = lax.psum(change, ('row', 'col'))  19 us
    all_gather x3, blocking collectives, local(): column_vec = lax.all_gather(scaled_own, 'row', axis=1, tiled=True)  10.5 us
    dot_general x3, matrix products, block_terms(): jnp.einsum('sij,sj->si', values, picked, preferred_element_type=jnp.float32)  10.1 us
    ppermute x3, starting transfers between devices, with_halo(): before = lax.ppermute(last, axis, up)  9.59 us
    reduce_sum x3, other arithmetic, local(): jnp.sum(ranks_now / own_denominator, axis=(1, 2, 3))  5.25 us
  transfers between devices with their start and end apart: 10, of which 4 were waited for; matrix products, arithmetic and copies ran while one was open for 0% of the time, Pallas kernels for 0%

commit v1 on v0

--- a/solution.py
+++ b/solution.py
@@ -1,3 +1,4 @@
+import functools
 import jax
 import jax.numpy as jnp
 from jax import lax
@@ -6,6 +7,13 @@
 ITERS = 3
 damping = 0.85
 coupling = 0.3
+
+
+def perform_digits_for(x0, ax_name):
+    return jnp.sum(jax.lax.all_gather(x0, axis_name=ax_name), axis=0)
+
+
+spread_space_here = functools.partial(perform_digits_for, ax_name="col")
 
 
 def with_halo(x, sides, width):
@@ -85,7 +93,7 @@
             layer_walk(values[0], block_row[0], block_col[0], live_slot[0], scaled[0], row_blk)
         ]
         partial_value = jnp.stack(layer_terms).reshape(layer_dev, 1, col_devices, span_len)
-        whole = lax.psum(partial_value, "col")
+        whole = spread_space_here(partial_value)
         walk_sum = lax.dynamic_slice_in_dim(whole, lax.axis_index("col"), 1, 2)
         updated = damping * (
             (1.0 - coupling) * (walk_sum + dangle_mass.reshape(layer_dev, 1, 1, 1) / node_total)

time: 199 us -> 178 us (0.89)
  waiting for transfers between devices: 53.8 us -> 35.2 us
  blocking collectives: 81.3 us -> 77.4 us
    psum x3 -> x0, waiting for transfers between devices: 33.3 us -> none  [local(): whole = lax.psum(partial_value, 'col')]
    all_gather x0 -> x3, waiting for transfers between devices: none -> 14.7 us  [perform_digits_for(): return jnp.sum(jax.lax.all_gather(x0, axis_name=ax_name), axis=0)]
    reduce_sum x0 -> x3, other arithmetic: none -> 4.4 us  [perform_digits_for(): return jnp.sum(jax.lax.all_gather(x0, axis_name=ax_name), axis=0)]
    all_gather x3, blocking collectives: 10.5 us -> 7.1 us  [local(): column_vec = lax.all_gather(scaled_own, 'row', axis=1, tiled=True)]
    psum x1, blocking collectives: 19 us -> 16.7 us  [local(): change_total = lax.psum(change, ('row', 'col'))]
  transfers between devices with their start and end apart: 10 -> 10, of which waited for: 4 -> 4; matrix products, arithmetic and copies ran while one was open for 0% -> 3% of each run, Pallas kernels for 0% -> 0%
where the time goes in v1:
time: 178 us; the launch traced here: 177 us
  blocking collectives  77.4 us (43%)
  waiting for transfers between devices  35.2 us (20%)
  between operations  16.7 us (9%)
  matrix products  14.8 us (8%)
  other arithmetic  13.9 us (8%)
  starting transfers between devices  13.7 us (8%)
  local copies, waits for them, and re-layouts  5.38 us (3%)
    psum x3, blocking collectives, local(): lax.psum(jnp.sum(ranks_now / own_denominator, axis=(1, 2, 3)), ('row', 'c...  53.7 us
    psum x1, waiting for transfers between devices, local(): degree = lax.psum(deg_part, 'row')  20.4 us
    psum x1, blocking collectives, local(): change_total = lax.psum(change, ('row', 'col'))  16.7 us
    all_gather x3, waiting for transfers between devices, perform_digits_for(): return jnp.sum(jax.lax.all_gather(x0, axis_name=ax_name), axis=0)  14.7 us
    dot_general x3, matrix products, block_terms(): jnp.einsum('sij,sj->si', values, picked, preferred_element_type=jnp.float32)  10.1 us
    ppermute x3, starting transfers between devices, with_halo(): before = lax.ppermute(last, axis, up)  9.67 us
    all_gather x3, blocking collectives, local(): column_vec = lax.all_gather(scaled_own, 'row', axis=1, tiled=True)  7.1 us
    reduce_sum x3, other arithmetic, perform_digits_for(): return jnp.sum(jax.lax.all_gather(x0, axis_name=ax_name), axis=0)  4.4 us
  transfers between devices with their start and end apart: 10, of which 4 were waited for; matrix products, arithmetic and copies ran while one was open for 3% of the time, Pallas kernels for 0%

profile of v1, /device:TPU:1, one launch (start us, length us, event | category | flops | bytes accessed | tf_op | source)
XLA Modules:
  0.0 177.1 jit_solution(1034075664587487139)
XLA Ops:
  7.9 2.8 %fusion.6 = f32[1,32,256]{2,0,1:T(1,128)S(1)} fusion(bf16[1,1,1,32,256,256]{5,4,3,2,1,0:T(8,128)(2,1)} %param.8), kind=kOutput, calls=%fused_computation.9 | convolution fusion | flops 4194304 | bytes 4227072 | tf_op jit(solution)/shard_map/lsij,i->lsj/dot_general | solution.py:61
  12.1 20.4 %all-reduce.3.cloned.1.call-done = f32[1,2,1,16384]{3,2,0,1:T(1,128)} async-done(((f32[1,2,1,16384]{3,2,0,1:T(1,128)}), f32[1,2,1,16384]{3,2,0,1:T(1,128)}) %all-reduce.3.cloned.1.call-update) | async-done | bytes 131088 | tf_op jit(solution)/shard_map/psum | solution.py:72
  32.6 1.6 fusion.20
  34.3 1.9 %all_gather.18 = bf16[1,2,1,16384]{3,2,0,1:T(2,128)(2,1)S(1)} all-gather(bf16[1,1,1,16384]{3,2,0,1:T(2,128)(2,1)S(1)} %fusion.23), channel_id=1, replica_groups=mesh['layer'=4,'row'=2,'col'=4] {'row'}, dimensions={1}, use_global_device_ids=true | all-gather | bytes 98304 | tf_op jit(solution)/shard_map/all_gather | solution.py:89
  37.3 3.4 %fusion.4 = f32[32,1,256]{2,1,0:T(1,128)S(1)} fusion(bf16[1,1,1,32,256,256]{5,4,3,2,1,0:T(8,128)(2,1)} %param.8, bf16[32,256,1]{1,0,2:T(8,128)(2,1)S(1)} %select_bitcast_fusion.2), kind=kOutput, calls=%fused_computation.7 | convolution fusion | flops 4194304 | bytes 4243456 | tf_op jit(solution)/shard_map/sij,sj->si/dot_general | solution.py:34
  42.2 3.4 %collective-permute-start = (bf16[1,1,1,16384]{3,2,0,1:T(2,128)(2,1)S(1)}, bf16[1,1,1,16384]{3,2,0,1:T(2,128)(2,1)S(1)}, u32[]{:S(2)}, u32[]{:S(2)}) collective-permute-start(bf16[1,1,1,16384]{3,2,0,1:T(2,128)(2,1)S(1)} %bitcast_convert_fusion), channel_id=1, source_target_pairs={{0,8},{8,16},{16,24},{1,9},{9,17},{17,25},{2,10},{10,18},{18,26},{... | collective-permute-start | bytes 98312 | tf_op jit(solution)/shard_map/ppermute | solution.py:26
  46.9 18.9 %psum.50 = f32[1]{0:T(128)} all-reduce(f32[1]{0:T(128)} %bitcast.10), channel_id=1, replica_groups=mesh['layer'=4,'row'=2,'col'=4] {'row','col'}, use_global_device_ids=true, to_apply=%region_3.5 | all-reduce | flops 1 | bytes 8 | tf_op jit(solution)/shard_map/psum | solution.py:90
  66.5 4.6 %all-gather.4.cloned.1.call-done = f32[4,1,1,4,16384]{4,3,2,1,0:T(4,128)} async-done(((f32[1,1,1,4,16384]{4,3,2,1,0:T(4,128)}), f32[4,1,1,4,16384]{4,3,2,1,0:T(4,128)}) %all-gather.4.cloned.1.call-update) | async-done | bytes 1048592 | tf_op jit(solution)/shard_map/all_gather | solution.py:13
  71.1 1.5 reduce_sum.93
  73.6 2.6 %all_gather.20 = bf16[1,2,1,16384]{3,2,0,1:T(2,128)(2,1)S(1)} all-gather(bf16[1,1,1,16384]{3,2,0,1:T(2,128)(2,1)S(1)} %get-tuple-element.22), channel_id=1, replica_groups=mesh['layer'=4,'row'=2,'col'=4] {'row'}, dimensions={1}, use_global_device_ids=true | all-gather | bytes 98304 | tf_op jit(solution)/shard_map/all_gather | solution.py:89
  77.4 3.4 %fusion.2 = f32[32,1,256]{2,1,0:T(1,128)S(1)} fusion(bf16[1,1,1,32,256,256]{5,4,3,2,1,0:T(8,128)(2,1)} %param.8, bf16[32,256,1]{1,0,2:T(8,128)(2,1)S(1)} %select_bitcast_fusion.1), kind=kOutput, calls=%fused_computation.5 | convolution fusion | flops 4194304 | bytes 4243456 | tf_op jit(solution)/shard_map/sij,sj->si/dot_general | solution.py:34
  82.2 3.3 %collective-permute-start.2 = (bf16[1,1,1,16384]{3,2,0,1:T(2,128)(2,1)S(1)}, bf16[1,1,1,16384]{3,2,0,1:T(2,128)(2,1)S(1)}, u32[]{:S(2)}, u32[]{:S(2)}) collective-permute-start(bf16[1,1,1,16384]{3,2,0,1:T(2,128)(2,1)S(1)} %get-tuple-element.23), channel_id=1, source_target_pairs={{0,8},{8,16},{16,24},{1,9},{9,17},{17,25},{2,10},{10,18},{18,26},{... | collective-permute-start | bytes 98312 | tf_op jit(solution)/shard_map/ppermute | solution.py:26
  86.8 17.4 %psum.51 = f32[1]{0:T(128)} all-reduce(f32[1]{0:T(128)} %bitcast.17), channel_id=1, replica_groups=mesh['layer'=4,'row'=2,'col'=4] {'row','col'}, use_global_device_ids=true, to_apply=%region_6.8 | all-reduce | flops 1 | bytes 8 | tf_op jit(solution)/shard_map/psum | solution.py:90
  104.9 4.9 %all-gather.6.cloned.1.call-done = f32[4,1,1,4,16384]{4,3,2,1,0:T(4,128)} async-done(((f32[1,1,1,4,16384]{4,3,2,1,0:T(4,128)}), f32[4,1,1,4,16384]{4,3,2,1,0:T(4,128)}) %all-gather.6.cloned.1.call-update) | async-done | bytes 1048592 | tf_op jit(solution)/shard_map/all_gather | solution.py:13
  109.7 1.5 reduce_sum.96
  112.2 2.6 %all_gather.22 = bf16[1,2,1,16384]{3,2,0,1:T(2,128)(2,1)S(1)} all-gather(bf16[1,1,1,16384]{3,2,0,1:T(2,128)(2,1)S(1)} %get-tuple-element.20), channel_id=1, replica_groups=mesh['layer'=4,'row'=2,'col'=4] {'row'}, dimensions={1}, use_global_device_ids=true | all-gather | bytes 98304 | tf_op jit(solution)/shard_map/all_gather | solution.py:89
  116.0 3.4 %fusion = f32[32,1,256]{2,1,0:T(1,128)S(1)} fusion(bf16[1,1,1,32,256,256]{5,4,3,2,1,0:T(8,128)(2,1)} %param.8, bf16[32,256,1]{1,0,2:T(8,128)(2,1)S(1)} %select_bitcast_fusion), kind=kOutput, calls=%fused_computation.3 | convolution fusion | flops 4194304 | bytes 4243456 | tf_op jit(solution)/shard_map/sij,sj->si/dot_general | solution.py:34
  120.8 3.0 %collective-permute-start.4 = (bf16[1,1,1,16384]{3,2,0,1:T(2,128)(2,1)S(1)}, bf16[1,1,1,16384]{3,2,0,1:T(2,128)(2,1)S(1)}, u32[]{:S(2)}, u32[]{:S(2)}) collective-permute-start(bf16[1,1,1,16384]{3,2,0,1:T(2,128)(2,1)S(1)} %get-tuple-element.21), channel_id=1, source_target_pairs={{0,8},{8,16},{16,24},{1,9},{9,17},{17,25},{2,10},{10,18},{18,26},{... | collective-permute-start | bytes 98312 | tf_op jit(solution)/shard_map/ppermute | solution.py:26
  125.1 17.3 %psum.52 = f32[1]{0:T(128)} all-reduce(f32[1]{0:T(128)} %bitcast.22), channel_id=1, replica_groups=mesh['layer'=4,'row'=2,'col'=4] {'row','col'}, use_global_device_ids=true, to_apply=%region_9.11 | all-reduce | flops 1 | bytes 8 | tf_op jit(solution)/shard_map/psum | solution.py:90
  143.1 5.2 %all-gather.8.cloned.1.call-done = f32[4,1,1,4,16384]{4,3,2,1,0:T(4,128)} async-done(((f32[1,1,1,4,16384]{4,3,2,1,0:T(4,128)}), f32[4,1,1,4,16384]{4,3,2,1,0:T(4,128)}) %all-gather.8.cloned.1.call-update) | async-done | bytes 1048592 | tf_op jit(solution)/shard_map/all_gather | solution.py:13
  148.2 1.5 reduce_sum.99
  149.7 1.7 fusion.19
  151.4 16.7 %all-reduce = (f32[1,1]{0,1:T(1,128)}, f32[1,1]{0,1:T(1,128)}, f32[1,1]{0,1:T(1,128)}) all-reduce(f32[1,1]{0,1:T(1,128)} %bitcast.29, f32[1,1]{0,1:T(1,128)} %bitcast.28, f32[1,1]{0,1:T(1,128)} %bitcast.27), channel_id=1, replica_groups=mesh['layer'=4,'row'=2,'col'=4] {'row','col'}, use_global_device_ids=true, to_apply=%region_15.17 | all-reduce | flops 3 | bytes 24 | tf_op jit(solution)/shard_map/psum | solution.py:103
  168.1 2.4 %pad_maximum_fusion.6 = f32[3,1]{0,1:T(1,128)} fusion(f32[1,1]{0,1:T(1,128)} %get-tuple-element.10, f32[1,1]{0,1:T(1,128)} %get-tuple-element.11, f32[1,1]{0,1:T(1,128)} %get-tuple-element.12), kind=kLoop, calls=%fused_computation.90 | loop fusion | flops 6 | bytes 24 | tf_op jit(solution)/shard_map/stack | solution.py:106
  (55 shorter events, 15.1 us)
Async XLA Ops:
  7.2 3.6 %copy-start.3 = (s32[1,1,1,32]{3,2,1,0:T(1,128)S(1)}, s32[1,1,1,32]{3,2,1,0:T(1,128)}, u32[]{:S(2)}) copy-start(s32[1,1,1,32]{3,2,1,0:T(1,128)} %param.10) | copy-start | bytes 388
  7.2 25.4 %copy-start = (s32[1,1,1,16384]{3,2,1,0:T(1,128)S(1)}, s32[1,1,1,16384]{3,2,1,0:T(1,128)}, u32[]{:S(2)}) copy-start(s32[1,1,1,16384]{3,2,1,0:T(1,128)} %param.12) | copy-start | bytes 196612
  7.2 25.4 %copy-start.1 = (f32[1,1,1,16384]{3,2,1,0:T(1,128)S(1)}, f32[1,1,1,16384]{3,2,1,0:T(1,128)}, u32[]{:S(2)}) copy-start(f32[1,1,1,16384]{3,2,1,0:T(1,128)} %param.13) | copy-start | bytes 196612
  7.2 25.4 %all-reduce.3.cloned.1.call-start = ((), (), s32[]{:S(2)}) async-start(), calls=%async_computation | async-start | bytes 262144 | tf_op jit(solution)/shard_map/psum | solution.py:72
  7.9 32.8 %copy-start.2 = (s32[1,1,1,32]{3,2,1,0:T(1,128)S(1)}, s32[1,1,1,32]{3,2,1,0:T(1,128)}, u32[]{:S(2)}) copy-start(s32[1,1,1,32]{3,2,1,0:T(1,128)} %param.9) | copy-start | bytes 388
  12.0 59.1 %all-gather.4.cloned.1.call-start = ((), (), s32[]{:S(2)}) async-start(), calls=%async_computation.1 | async-start | bytes 1310720 | tf_op jit(solution)/shard_map/all_gather | solution.py:13
  42.1 67.6 %all-gather.6.cloned.1.call-start = ((), (), s32[]{:S(2)}) async-start(), calls=%async_computation.2 | async-start | bytes 1310720 | tf_op jit(solution)/shard_map/all_gather | solution.py:13
  42.2 30.3 %collective-permute-start = (bf16[1,1,1,16384]{3,2,0,1:T(2,128)(2,1)S(1)}, bf16[1,1,1,16384]{3,2,0,1:T(2,128)(2,1)S(1)}, u32[]{:S(2)}, u32[]{:S(2)}) collective-permute-start(bf16[1,1,1,16384]{3,2,0,1:T(2,128)(2,1)S(1)} %bitcast_convert_fusion), channel_id=1, source_target_pairs={{0,8},{8,16},{16,24},{1,9},{9,17},{17,25},{2,10},{10,18},{18,26},{... | collective-permute-start | bytes 98312 | tf_op jit(solution)/shard_map/ppermute | solution.py:26
  45.6 27.0 %collective-permute-start.1 = (bf16[1,1,1,16384]{3,2,0,1:T(2,128)(2,1)S(1)}, bf16[1,1,1,16384]{3,2,0,1:T(2,128)(2,1)S(1)}, u32[]{:S(2)}, u32[]{:S(2)}) collective-permute-start(bf16[1,1,1,16384]{3,2,0,1:T(2,128)(2,1)S(1)} %bitcast_convert_fusion), channel_id=1, source_target_pairs={{8,0},{16,8},{24,16},{9,1},{17,9},{25,17},{10,2},{18,10},{26,18},{... | collective-permute-start | bytes 98312 | tf_op jit(solution)/shard_map/ppermute | solution.py:27
  82.1 66.1 %all-gather.8.cloned.1.call-start = ((), (), s32[]{:S(2)}) async-start(), calls=%async_computation.3 | async-start | bytes 1310720 | tf_op jit(solution)/shard_map/all_gather | solution.py:13
  82.2 29.0 %collective-permute-start.2 = (bf16[1,1,1,16384]{3,2,0,1:T(2,128)(2,1)S(1)}, bf16[1,1,1,16384]{3,2,0,1:T(2,128)(2,1)S(1)}, u32[]{:S(2)}, u32[]{:S(2)}) collective-permute-start(bf16[1,1,1,16384]{3,2,0,1:T(2,128)(2,1)S(1)} %get-tuple-element.23), channel_id=1, source_target_pairs={{0,8},{8,16},{16,24},{1,9},{9,17},{17,25},{2,10},{10,18},{18,26},{... | collective-permute-start | bytes 98312 | tf_op jit(solution)/shard_map/ppermute | solution.py:26
  85.5 25.7 %collective-permute-start.3 = (bf16[1,1,1,16384]{3,2,0,1:T(2,128)(2,1)S(1)}, bf16[1,1,1,16384]{3,2,0,1:T(2,128)(2,1)S(1)}, u32[]{:S(2)}, u32[]{:S(2)}) collective-permute-start(bf16[1,1,1,16384]{3,2,0,1:T(2,128)(2,1)S(1)} %get-tuple-element.23), channel_id=1, source_target_pairs={{8,0},{16,8},{24,16},{9,1},{17,9},{25,17},{10,2},{18,10},{26,18},{... | collective-permute-start | bytes 98312 | tf_op jit(solution)/shard_map/ppermute | solution.py:27
  120.8 28.9 %collective-permute-start.4 = (bf16[1,1,1,16384]{3,2,0,1:T(2,128)(2,1)S(1)}, bf16[1,1,1,16384]{3,2,0,1:T(2,128)(2,1)S(1)}, u32[]{:S(2)}, u32[]{:S(2)}) collective-permute-start(bf16[1,1,1,16384]{3,2,0,1:T(2,128)(2,1)S(1)} %get-tuple-element.21), channel_id=1, source_target_pairs={{0,8},{8,16},{16,24},{1,9},{9,17},{17,25},{2,10},{10,18},{18,26},{... | collective-permute-start | bytes 98312 | tf_op jit(solution)/shard_map/ppermute | solution.py:26
  123.8 26.0 %collective-permute-start.5 = (bf16[1,1,1,16384]{3,2,0,1:T(2,128)(2,1)S(1)}, bf16[1,1,1,16384]{3,2,0,1:T(2,128)(2,1)S(1)}, u32[]{:S(2)}, u32[]{:S(2)}) collective-permute-start(bf16[1,1,1,16384]{3,2,0,1:T(2,128)(2,1)S(1)} %get-tuple-element.21), channel_id=1, source_target_pairs={{8,0},{16,8},{24,16},{9,1},{17,9},{25,17},{10,2},{18,10},{26,18},{... | collective-permute-start | bytes 98312 | tf_op jit(solution)/shard_map/ppermute | solution.py:27
Sparse Core Ops, SparseCore 0:
  12.1 20.3 all-reduce.2
  42.2 28.8 all-gather.3
  82.3 27.4 all-gather.5
  120.9 27.2 all-gather.7
